TPU v7x, 32 devices: a 4x4x1 block of a 4x4x8 slice. The times are simulated.
32 devices in a mesh: batch: 1 (over z), cy: 4 (over y), cx: 8 (over x, core).
Axes of the slice: x: 4, y: 4, z: 1, core: 2. Of those that a mesh axis runs over, the one named last changes fastest.
The devices are a block of a 4x4x8 slice.
Arguments:
- q_seq: bfloat16 [4096, 32, 64], P(('batch', 'cx', 'cy'))
- k_seq: bfloat16 [4096, 8, 64], P(('batch', 'cx', 'cy'))
- v_seq: bfloat16 [4096, 8, 64], P(('batch', 'cx', 'cy'))
Outputs:
- output: bfloat16 [4096, 32, 64], P(('batch', 'cx', 'cy'))
All inputs are finite; a program needn't handle non-finite values.
Results may differ from a plain program's by a relative error of at most 0.00508428.
Values are sent between devices in bfloat16 or wider.
A program may use at most 768 MiB of HBM per device.

v0:
```python
import functools
import math

import jax
import jax.numpy as jnp
from jax import lax
from jax.experimental import pallas as pl
from jax.experimental.pallas import tpu as pltpu
from jax.sharding import PartitionSpec as P

F32 = jnp.float32
BF16 = jnp.bfloat16
MESH = pl.DeviceIdType.MESH

TILE = 256
MEMBERS = 8
BLOCKS = 4
GROUPS = (
    ((0, 0),),
    ((1, 0),),
    ((4, 0),),
    ((2, 0),),
    ((5, 0), (3, 0)),
    ((4, 1), (2, 1), (5, 1)),
    ((3, 1), (6, 0), (7, 0), (7, 1), (6, 1)),
    ((7, 2), (6, 2), (7, 3), (6, 3)),
    ((5, 2), (5, 3), (3, 2), (3, 3)),
    ((4, 2), (4, 3), (2, 2), (2, 3)),
    ((1, 1), (1, 2), (1, 3)),
    ((0, 1), (0, 2), (0, 3)),
)
KEYS, VALUES = 0, 1
RELAYS = {3: ((KEYS, 1),), 4: ((KEYS, 2),), 5: ((VALUES, 1), (VALUES, 2))}


def flip(value):
    return value + 1 - 2 * lax.rem(value, 2)


def attend_kernel(
    size_x, size_y, scale,
    q_hbm, k_hbm, v_hbm, out_ref,
    q_ref, k_ref, v_ref, q_got, kv_got, keys, q_limbs, scores, block_max, row_max, row_sum, acc, out_send,
    staged, kv_sent, kv_here, q_sent, q_here, fwd_sent, fwd_here, out_sent, out_here,
):
    head_dim, tokens = k_ref.shape[1:]
    group = q_ref.shape[0] // k_ref.shape[0]
    tiles = group * tokens // TILE
    per_tile = TILE // tokens
    span = MEMBERS * tokens

    local = [pltpu.make_async_copy(*pair, staged.at[n]) for n, pair in
             enumerate(((k_hbm, k_ref), (v_hbm, v_ref), (q_hbm, q_ref)))]
    for copy in local:
        copy.start()

    ix = lax.axis_index("cx")
    iy = lax.axis_index("cy")
    chips_x = size_x // 2
    chip_x, core = ix // 2, lax.rem(ix, 2)
    half_x, half_y = chips_x // 2, size_y // 2

    def head_of(x, y, c):
        px = lax.rem(x + x // half_x, 2)
        py = lax.rem(y + y // half_y, 2)
        return px * 4 + py * 2 + c

    def member(r):
        x = flip(chip_x) if r // 4 else chip_x
        y = flip(iy) if (r // 2) % 2 else iy
        c = flip(core) if r % 2 else core
        return {"cx": x * 2 + c, "cy": y}, head_of(x, y, c)

    my_head = head_of(chip_x, iy, core)
    mirror_x = {"cx": (chips_x - 1 - chip_x) * 2 + core, "cy": iy}
    mirror_y = {"cx": ix, "cy": size_y - 1 - iy}

    barrier = pltpu.get_barrier_semaphore()
    partners = [member(r)[0] for r in range(1, MEMBERS)] + [mirror_x, mirror_y]
    for who in partners:
        pl.semaphore_signal(barrier, inc=1, device_id=who, device_id_type=MESH)
    pl.semaphore_wait(barrier, len(partners))

    def remote(src, dst, sent, here, who):
        return pltpu.make_async_remote_copy(
            src_ref=src, dst_ref=dst, send_sem=sent, recv_sem=here, device_id=who, device_id_type=MESH
        )

    def kv_copy(kind, r):
        who, head = member(r)
        src = (k_ref, v_ref)[kind].at[head]
        return remote(src, kv_got.at[kind, 0, r], kv_sent.at[kind, r], kv_here.at[kind, r], who)

    def q_copy(r):
        who, head = member(r)
        return remote(q_ref.at[pl.ds(head * group, group)], q_got.at[r], q_sent.at[r], q_here.at[r], who)

    def forward(kind, block, r):
        index = (block - 1) * MEMBERS + r
        if block == 3:
            src, who = (kv_got.at[kind, 1, r], mirror_y) if r < 4 else (kv_got.at[kind, 2, r], mirror_x)
        else:
            src = kv_got.at[kind, 0, r] if r else (k_ref, v_ref)[kind].at[my_head]
            who = mirror_x if block == 1 else mirror_y
        return remote(src, kv_got.at[kind, block, r], fwd_sent.at[kind, index], fwd_here.at[kind, index], who)

    def out_copy(r, head):
        return remote(
            out_send.at[r], out_ref.at[pl.ds(head * group, group)], out_sent.at[r], out_here.at[r], member(r)[0]
        )

    for kind in (KEYS, VALUES):
        local[kind].wait()
        for r in range(1, MEMBERS):
            kv_copy(kind, r).start()
        forward(kind, 1, 0).start()
        forward(kind, 2, 0).start()
    local[2].wait()
    for r in (1, 4, 2, 5, 3, 6, 7):
        q_copy(r).start()

    def prepare_keys(block, r, columns):
        base = block * span + r * tokens
        keys[pl.ds(base, tokens)] = jnp.transpose(jnp.concatenate([columns, columns], axis=0))

    def prepare_queries(r, read):
        for g in range(group):
            wide = read(g).astype(F32) * scale
            high = wide.astype(BF16)
            rest = wide - high.astype(F32)
            middle = rest.astype(BF16)
            low = (rest - middle.astype(F32)).astype(BF16)
            cols = pl.ds(g % per_tile * tokens, tokens)
            for n, term in enumerate((high, middle, low)):
                q_limbs[r, g // per_tile, pl.ds(n * head_dim, head_dim), cols] = term

    def score(r, b):
        doubled = keys[pl.ds(b * span, span)]
        lhs = jnp.concatenate([doubled, doubled], axis=1)
        for t in range(tiles):
            s = jnp.dot(lhs, q_limbs[r, t], preferred_element_type=F32)
            scores[t] = s
            block_max[t] = jnp.max(s.reshape(span // 8, 8, TILE), axis=0)

    def step(r, b, following):
        probs, factors = [], []
        for t in range(tiles):
            old = row_max[r, t]
            new = jnp.maximum(old, jnp.max(block_max[t], axis=0, keepdims=True))
            row_max[r, t] = new
            factors.append(jnp.exp2(old - new))
            p = jnp.exp2(scores[t].reshape(span // 8, 8, TILE) - new[None])
            row_sum[r, t] = row_sum[r, t] * factors[t] + jnp.sum(p, axis=0)
            probs.append(p.reshape(span, TILE).astype(BF16))
        if following:
            score(*following)
        values = jnp.concatenate([kv_got[VALUES, b, m] for m in range(MEMBERS)], axis=1)
        for t in range(tiles):
            weighted = jnp.dot(values, probs[t], preferred_element_type=F32)
            acc[r, t] = acc[r, t] * factors[t][0:1] + weighted

    def finish(r):
        for t in range(tiles):
            inverse = 1.0 / jnp.sum(row_sum[r, t], axis=0, keepdims=True)
            result = (acc[r, t] * inverse).astype(BF16)
            for n in range(per_tile):
                out_send[r, t * per_tile + n] = result[:, n * tokens:(n + 1) * tokens]

    row_max[...] = jnp.full_like(row_max, -jnp.inf)
    row_sum[...] = jnp.zeros_like(row_sum)
    acc[...] = jnp.zeros_like(acc)
    q_limbs[:, :, pl.ds(3 * head_dim, TILE - 3 * head_dim)] = jnp.zeros(
        (MEMBERS, tiles, TILE - 3 * head_dim, TILE), BF16
    )
    prepare_queries(0, lambda g: q_ref[my_head * group + g])
    prepare_keys(0, 0, k_ref[my_head])
    kv_got[VALUES, 0, 0] = v_ref[my_head]

    def values_here(m):
        kv_copy(VALUES, m).wait_recv()
        forward(VALUES, 1, m).start()
        forward(VALUES, 2, m).start()

    for some in ((1,), (2, 3, 4, 5), (6, 7)):
        for r in some:
            kv_copy(KEYS, r).wait_recv()
            forward(KEYS, 1, r).start()
            forward(KEYS, 2, r).start()
            if r == 1:
                values_here(r)
        for r in some:
            prepare_keys(0, r, kv_got[KEYS, 0, r])

    ready_q, ready_k, ready_v = {0}, {0}, set()

    def relayed(block, r):
        return (block, r // 4) in ((1, 0), (2, 1))

    def relay(kind, block):
        for m in range(MEMBERS):
            if relayed(block, m):
                forward(kind, block, m).wait_recv()
                forward(kind, 3, m).start()

    def require_scores(r, b):
        if r not in ready_q:
            ready_q.add(r)
            q_copy(r).wait_recv()
            prepare_queries(r, lambda g: q_got[r, g])
        if b not in ready_k:
            ready_k.add(b)
            for m in range(MEMBERS):
                if not relayed(b, m):
                    forward(KEYS, b, m).wait_recv()
            for m in range(MEMBERS):
                prepare_keys(b, m, kv_got[KEYS, b, m])

    def require_values(b):
        if b not in ready_v:
            ready_v.add(b)
            for m in range(MEMBERS):
                if b and not relayed(b, m):
                    forward(VALUES, b, m).wait_recv()
                if not b and m > 1:
                    values_here(m)

    order = [step for group in GROUPS for step in group]
    last = {r: n for n, (r, b) in enumerate(order)}
    score(*order[0])
    n = 0
    ended = []
    for number, members in enumerate(GROUPS):
        for kind, block in RELAYS.get(number, ()):
            relay(kind, block)
        for following in order[n + 1:n + len(members) + 1]:
            require_scores(*following)
        for r, b in members:
            require_values(b)
        for r in ended:
            out_copy(r, my_head).start()
        ended = []
        for r, b in members:
            step(r, b, order[n + 1] if n + 1 < len(order) else None)
            if last[r] == n:
                finish(r)
                ended += [r] if r else []
            n += 1
    mine = pltpu.make_async_copy(out_send.at[0], out_ref.at[pl.ds(my_head * group, group)], out_sent.at[0])
    mine.start()

    for r in range(1, MEMBERS):
        out_copy(r, member(r)[1]).wait_recv()
        out_copy(r, my_head).wait_send()
        q_copy(r).wait_send()
    for kind in (KEYS, VALUES):
        for r in range(1, MEMBERS):
            kv_copy(kind, r).wait_send()
        for block in range(1, BLOCKS):
            for r in range(MEMBERS):
                forward(kind, block, r).wait_send()
    mine.wait()


def solution(mesh):
    size_x = mesh.shape["cx"]
    size_y = mesh.shape["cy"]
    seq_spec = P(("batch", "cx", "cy"), None, None)

    def local_attention(q_local, k_local, v_local):
        tokens, num_heads, head_dim = q_local.shape
        num_kv = k_local.shape[1]
        group = num_heads // num_kv
        tiles = group * tokens // TILE
        span = MEMBERS * tokens
        scale = 1.0 / math.sqrt(head_dim) / math.log(2.0)
        hbm = pl.BlockSpec(memory_space=pl.ANY)
        out_cols = pl.pallas_call(
            functools.partial(attend_kernel, size_x, size_y, scale),
            out_shape=jax.ShapeDtypeStruct((num_heads, head_dim, tokens), BF16),
            in_specs=[hbm] * 3,
            out_specs=hbm,
            scratch_shapes=[
                pltpu.VMEM((num_heads, head_dim, tokens), BF16),
                pltpu.VMEM((num_kv, head_dim, tokens), BF16),
                pltpu.VMEM((num_kv, head_dim, tokens), BF16),
                pltpu.VMEM((MEMBERS, group, head_dim, tokens), BF16),
                pltpu.VMEM((2, BLOCKS, MEMBERS, head_dim, tokens), BF16),
                pltpu.VMEM((BLOCKS * span, 2 * head_dim), BF16),
                pltpu.VMEM((MEMBERS, tiles, TILE, TILE), BF16),
                pltpu.VMEM((tiles, span, TILE), F32),
                pltpu.VMEM((tiles, 8, TILE), F32),
                pltpu.VMEM((MEMBERS, tiles, 8, TILE), F32),
                pltpu.VMEM((MEMBERS, tiles, 8, TILE), F32),
                pltpu.VMEM((MEMBERS, tiles, head_dim, TILE), F32),
                pltpu.VMEM((MEMBERS, group, head_dim, tokens), BF16),
                pltpu.SemaphoreType.DMA((3,)),
                pltpu.SemaphoreType.DMA((2, MEMBERS)),
                pltpu.SemaphoreType.DMA((2, MEMBERS)),
                pltpu.SemaphoreType.DMA((MEMBERS,)),
                pltpu.SemaphoreType.DMA((MEMBERS,)),
                pltpu.SemaphoreType.DMA((2, (BLOCKS - 1) * MEMBERS)),
                pltpu.SemaphoreType.DMA((2, (BLOCKS - 1) * MEMBERS)),
                pltpu.SemaphoreType.DMA((MEMBERS,)),
                pltpu.SemaphoreType.DMA((MEMBERS,)),
            ],
            compiler_params=pltpu.CompilerParams(
                collective_id=0,
                has_side_effects=True,
            ),
        )(*(jnp.transpose(x, (1, 2, 0)) for x in (q_local, k_local, v_local)))
        return jnp.transpose(out_cols, (2, 0, 1))

    return jax.shard_map(
        local_attention, mesh=mesh, in_specs=(seq_spec, seq_spec, seq_spec), out_specs=seq_spec, check_vma=False
    )
```

profile of v0, /device:TPU:97, one launch (start us, length us, event | category | flops | bytes accessed | tf_op | source)
XLA Modules:
  0.0 35.2 jit_solution(11710551838474690724)
XLA Ops:
  0.0 33.3 %shard_map.37 = bf16[32,64,128]{2,1,0:T(8,128)(2,1)} custom-call(bf16[32,64,128]{2,1,0:T(8,128)(2,1)} %bitcast.5, bf16[8,64,128]{2,1,0:T(8,128)(2,1)} %bitcast.6, bf16[8,64,128]{2,1,0:T(8,128)(2,1)} %bitcast.7), custom_call_target="tpu_custom_call" | custom-call | tf_op jit(solution)/shard_map/pallas_call | solution.py:277
  33.3 1.9 %copy.5 = bf16[128,32,64]{0,2,1:T(8,128)(2,1)} copy(bf16[128,32,64]{0,2,1:T(8,128)(2,1)} %bitcast.4) | data formatting | bytes 1048576
where the time goes:
time: 35.3 us; the launch traced here: 35.2 us
  Pallas kernels  33.3 us (94%)
  local copies, waits for them, and re-layouts  1.87 us (5%)
    pallas_call x1, Pallas kernels, local_attention(): pl.pallas_call(functools.partial(attend_kernel, size_x, size_y, scale), o...  33.3 us
    unnamed x1, local copies, waits for them, and re-layouts  1.87 us

commit v1 on v0

--- a/solution.py
+++ b/solution.py
@@ -15,22 +15,30 @@
 TILE = 256
 MEMBERS = 8
 BLOCKS = 4
+SETS = (
+    ((0, 0), (0, 1), (0, 2), (0, 3), (0, 4), (0, 5), (1, 0), (2, 0)),
+    ((1, 1), (2, 1), (1, 2), (1, 3), (2, 4), (2, 5), (0, 6), (0, 7)),
+    ((1, 4), (1, 5), (2, 2), (2, 3), (1, 6), (1, 7), (2, 6), (2, 7)),
+    tuple((3, r) for r in range(MEMBERS)),
+)
 GROUPS = (
     ((0, 0),),
     ((1, 0),),
     ((4, 0),),
     ((2, 0),),
-    ((5, 0), (3, 0)),
-    ((4, 1), (2, 1), (5, 1)),
-    ((3, 1), (6, 0), (7, 0), (7, 1), (6, 1)),
-    ((7, 2), (6, 2), (7, 3), (6, 3)),
+    ((4, 1), (2, 1)),
+    ((5, 0), (3, 0), (5, 1)),
+    ((3, 1),),
+    ((6, 0), (6, 1)),
+    ((6, 2), (7, 0), (7, 1), (7, 2)),
+    ((7, 3), (6, 3)),
     ((5, 2), (5, 3), (3, 2), (3, 3)),
     ((4, 2), (4, 3), (2, 2), (2, 3)),
     ((1, 1), (1, 2), (1, 3)),
     ((0, 1), (0, 2), (0, 3)),
 )
 KEYS, VALUES = 0, 1
-RELAYS = {3: ((KEYS, 1),), 4: ((KEYS, 2),), 5: ((VALUES, 1), (VALUES, 2))}
+RELAYS = {1: ((1, 0), (1, 1)), 4: ((1, 2), (1, 3), (2, 4), (2, 5)), 6: ((2, 6), (2, 7))}
 
 
 def flip(value):
@@ -109,18 +117,26 @@
             out_send.at[r], out_ref.at[pl.ds(head * group, group)], out_sent.at[r], out_here.at[r], member(r)[0]
         )
 
+    local[KEYS].wait()
+    local[VALUES].wait()
     for kind in (KEYS, VALUES):
-        local[kind].wait()
-        for r in range(1, MEMBERS):
-            kv_copy(kind, r).start()
         forward(kind, 1, 0).start()
         forward(kind, 2, 0).start()
+    for some in ((1,), (4, 2, 5, 3)):
+        for kind in (KEYS, VALUES):
+            for r in some:
+                kv_copy(kind, r).start()
     local[2].wait()
-    for r in (1, 4, 2, 5, 3, 6, 7):
+    for r in (1, 4, 2):
         q_copy(r).start()
-
-    def prepare_keys(block, r, columns):
-        base = block * span + r * tokens
+    for kind in (KEYS, VALUES):
+        for r in (6, 7):
+            kv_copy(kind, r).start()
+    for r in (5, 3, 6, 7):
+        q_copy(r).start()
+
+    def prepare_keys(number, slot, columns):
+        base = number * span + slot * tokens
         keys[pl.ds(base, tokens)] = jnp.transpose(jnp.concatenate([columns, columns], axis=0))
 
     def prepare_queries(r, read):
@@ -154,7 +170,7 @@
             probs.append(p.reshape(span, TILE).astype(BF16))
         if following:
             score(*following)
-        values = jnp.concatenate([kv_got[VALUES, b, m] for m in range(MEMBERS)], axis=1)
+        values = jnp.concatenate([kv_got[VALUES, block, m] for block, m in SETS[b]], axis=1)
         for t in range(tiles):
             weighted = jnp.dot(values, probs[t], preferred_element_type=F32)
             acc[r, t] = acc[r, t] * factors[t][0:1] + weighted
@@ -176,31 +192,24 @@
     prepare_keys(0, 0, k_ref[my_head])
     kv_got[VALUES, 0, 0] = v_ref[my_head]
 
-    def values_here(m):
-        kv_copy(VALUES, m).wait_recv()
-        forward(VALUES, 1, m).start()
-        forward(VALUES, 2, m).start()
-
-    for some in ((1,), (2, 3, 4, 5), (6, 7)):
-        for r in some:
-            kv_copy(KEYS, r).wait_recv()
-            forward(KEYS, 1, r).start()
-            forward(KEYS, 2, r).start()
-            if r == 1:
-                values_here(r)
-        for r in some:
-            prepare_keys(0, r, kv_got[KEYS, 0, r])
-
-    ready_q, ready_k, ready_v = {0}, {0}, set()
-
-    def relayed(block, r):
-        return (block, r // 4) in ((1, 0), (2, 1))
-
-    def relay(kind, block):
-        for m in range(MEMBERS):
-            if relayed(block, m):
-                forward(kind, block, m).wait_recv()
-                forward(kind, 3, m).start()
+    arrived = {(KEYS, 0, 0), (VALUES, 0, 0)}
+    ready_q, ready_k = {0}, set()
+
+    def arrive(kind, block, r):
+        if (kind, block, r) in arrived:
+            return
+        arrived.add((kind, block, r))
+        if block:
+            forward(kind, block, r).wait_recv()
+        else:
+            kv_copy(kind, r).wait_recv()
+            forward(kind, 1, r).start()
+            forward(kind, 2, r).start()
+
+    def relay(block, r):
+        for kind in (KEYS, VALUES):
+            arrive(kind, block, r)
+            forward(kind, 3, r).start()
 
     def require_scores(r, b):
         if r not in ready_q:
@@ -209,33 +218,31 @@
             prepare_queries(r, lambda g: q_got[r, g])
         if b not in ready_k:
             ready_k.add(b)
-            for m in range(MEMBERS):
-                if not relayed(b, m):
-                    forward(KEYS, b, m).wait_recv()
-            for m in range(MEMBERS):
-                prepare_keys(b, m, kv_got[KEYS, b, m])
+            for block, m in SETS[b]:
+                arrive(KEYS, block, m)
+            for slot, (block, m) in enumerate(SETS[b]):
+                if (block, m) != (0, 0):
+                    prepare_keys(b, slot, kv_got[KEYS, block, m])
 
     def require_values(b):
-        if b not in ready_v:
-            ready_v.add(b)
-            for m in range(MEMBERS):
-                if b and not relayed(b, m):
-                    forward(VALUES, b, m).wait_recv()
-                if not b and m > 1:
-                    values_here(m)
-
+        for block, m in SETS[b]:
+            arrive(VALUES, block, m)
+
+    arrive(KEYS, 0, 1)
+    arrive(VALUES, 0, 1)
+    require_scores(0, 0)
     order = [step for group in GROUPS for step in group]
     last = {r: n for n, (r, b) in enumerate(order)}
     score(*order[0])
     n = 0
     ended = []
     for number, members in enumerate(GROUPS):
-        for kind, block in RELAYS.get(number, ()):
-            relay(kind, block)
         for following in order[n + 1:n + len(members) + 1]:
             require_scores(*following)
         for r, b in members:
             require_values(b)
+        for piece in RELAYS.get(number, ()):
+            relay(*piece)
         for r in ended:
             out_copy(r, my_head).start()
         ended = []

time: 35.3 us -> 36.8 us (1.042)
  Pallas kernels: 33.3 us -> 34.7 us
    pallas_call x1, Pallas kernels: 33.3 us -> 34.7 us  [local_attention(): pl.pallas_call(functools.partial(attend_kernel, size_x, size_y, scale), o...]
where the time goes in v1:
time: 36.8 us; the launch traced here: 36.6 us
  Pallas kernels  34.7 us (94%)
  local copies, waits for them, and re-layouts  1.87 us (5%)
    pallas_call x1, Pallas kernels, local_attention(): pl.pallas_call(functools.partial(attend_kernel, size_x, size_y, scale), o...  34.7 us
    unnamed x1, local copies, waits for them, and re-layouts  1.87 us

profile of v1, /device:TPU:97, one launch (start us, length us, event | category | flops | bytes accessed | tf_op | source)
XLA Modules:
  0.0 36.6 jit_solution(3617522814951373980)
XLA Ops:
  0.0 34.7 %shard_map.37 = bf16[32,64,128]{2,1,0:T(8,128)(2,1)} custom-call(bf16[32,64,128]{2,1,0:T(8,128)(2,1)} %bitcast.5, bf16[8,64,128]{2,1,0:T(8,128)(2,1)} %bitcast.6, bf16[8,64,128]{2,1,0:T(8,128)(2,1)} %bitcast.7), custom_call_target="tpu_custom_call" | custom-call | tf_op jit(solution)/shard_map/pallas_call | solution.py:284
  34.7 1.9 %copy.5 = bf16[128,32,64]{0,2,1:T(8,128)(2,1)} copy(bf16[128,32,64]{0,2,1:T(8,128)(2,1)} %bitcast.4) | data formatting | bytes 1048576

commit v2 on v1

--- a/solution.py
+++ b/solution.py
@@ -25,20 +25,18 @@
     ((0, 0),),
     ((1, 0),),
     ((4, 0),),
-    ((2, 0),),
-    ((4, 1), (2, 1)),
-    ((5, 0), (3, 0), (5, 1)),
-    ((3, 1),),
-    ((6, 0), (6, 1)),
-    ((6, 2), (7, 0), (7, 1), (7, 2)),
-    ((7, 3), (6, 3)),
-    ((5, 2), (5, 3), (3, 2), (3, 3)),
-    ((4, 2), (4, 3), (2, 2), (2, 3)),
+    ((2, 0), (4, 1), (2, 1)),
+    ((5, 0), (3, 0), (5, 1), (3, 1)),
+    ((6, 0), (6, 1), (6, 2)),
+    ((7, 0), (7, 1), (7, 2), (5, 2)),
+    ((7, 3), (6, 3), (5, 3)),
+    ((3, 2), (3, 3), (4, 2), (4, 3)),
+    ((2, 2), (2, 3)),
     ((1, 1), (1, 2), (1, 3)),
     ((0, 1), (0, 2), (0, 3)),
 )
 KEYS, VALUES = 0, 1
-RELAYS = {1: ((1, 0), (1, 1)), 4: ((1, 2), (1, 3), (2, 4), (2, 5)), 6: ((2, 6), (2, 7))}
+RELAYS = {1: ((1, 0), (1, 1)), 3: ((1, 2), (1, 3), (2, 4), (2, 5)), 5: ((2, 6), (2, 7))}
 
 
 def flip(value):
@@ -180,7 +178,11 @@
             inverse = 1.0 / jnp.sum(row_sum[r, t], axis=0, keepdims=True)
             result = (acc[r, t] * inverse).astype(BF16)
             for n in range(per_tile):
-                out_send[r, t * per_tile + n] = result[:, n * tokens:(n + 1) * tokens]
+                part = result[:, n * tokens:(n + 1) * tokens]
+                if r:
+                    out_send[r, t * per_tile + n] = part
+                else:
+                    out_ref[my_head * group + t * per_tile + n] = part
 
     row_max[...] = jnp.full_like(row_max, -jnp.inf)
     row_sum[...] = jnp.zeros_like(row_sum)
@@ -252,9 +254,6 @@
                 finish(r)
                 ended += [r] if r else []
             n += 1
-    mine = pltpu.make_async_copy(out_send.at[0], out_ref.at[pl.ds(my_head * group, group)], out_sent.at[0])
-    mine.start()
-
     for r in range(1, MEMBERS):
         out_copy(r, member(r)[1]).wait_recv()
         out_copy(r, my_head).wait_send()
@@ -265,7 +264,12 @@
         for block in range(1, BLOCKS):
             for r in range(MEMBERS):
                 forward(kind, block, r).wait_send()
-    mine.wait()
+
+
+def store_kernel(result, out_ref, stored):
+    copy = pltpu.make_async_copy(result, out_ref, stored)
+    copy.start()
+    copy.wait()
 
 
 def solution(mesh):
@@ -281,11 +285,12 @@
         span = MEMBERS * tokens
         scale = 1.0 / math.sqrt(head_dim) / math.log(2.0)
         hbm = pl.BlockSpec(memory_space=pl.ANY)
+        vmem = pl.BlockSpec(memory_space=pltpu.VMEM)
         out_cols = pl.pallas_call(
             functools.partial(attend_kernel, size_x, size_y, scale),
-            out_shape=jax.ShapeDtypeStruct((num_heads, head_dim, tokens), BF16),
+            out_shape=pltpu.VMEM((num_heads, head_dim, tokens), BF16),
             in_specs=[hbm] * 3,
-            out_specs=hbm,
+            out_specs=vmem,
             scratch_shapes=[
                 pltpu.VMEM((num_heads, head_dim, tokens), BF16),
                 pltpu.VMEM((num_kv, head_dim, tokens), BF16),
@@ -315,6 +320,14 @@
                 has_side_effects=True,
             ),
         )(*(jnp.transpose(x, (1, 2, 0)) for x in (q_local, k_local, v_local)))
+        out_cols = pl.pallas_call(
+            store_kernel,
+            out_shape=jax.ShapeDtypeStruct(out_cols.shape, BF16),
+            in_specs=[vmem],
+            out_specs=hbm,
+            scratch_shapes=[pltpu.SemaphoreType.DMA],
+            compiler_params=pltpu.CompilerParams(vmem_limit_bytes=1024 * 1024),
+        )(pltpu.with_memory_space_constraint(out_cols, pltpu.VMEM))
         return jnp.transpose(out_cols, (2, 0, 1))
 
     return jax.shard_map(

time: 36.8 us -> 36.4 us (0.989)
  local copies, waits for them, and re-layouts: 1.87 us -> 0 us
  Pallas kernels: 34.7 us -> 36.2 us
    unnamed x1 -> x0, local copies, waits for them, and re-layouts: 1.87 us -> none
    pallas_call x0 -> x1, Pallas kernels: none -> 0.8 us  [local_attention(): pl.pallas_call(store_kernel, out_shape=jax.ShapeDtypeStruct(out_cols.shap...]
    pallas_call x1, Pallas kernels: 34.7 us -> 35.3 us  [local_attention(): pl.pallas_call(functools.partial(attend_kernel, size_x, size_y, scale), o...]
where the time goes in v2:
time: 36.4 us; the launch traced here: 36.3 us
  Pallas kernels  36.2 us (99%)
    pallas_call x1, Pallas kernels, local_attention(): pl.pallas_call(functools.partial(attend_kernel, size_x, size_y, scale), o...  35.3 us
    pallas_call x1, Pallas kernels, local_attention(): pl.pallas_call(store_kernel, out_shape=jax.ShapeDtypeStruct(out_cols.shap...  0.8 us

profile of v2, /device:TPU:97, one launch (start us, length us, event | category | flops | bytes accessed | tf_op | source)
XLA Modules:
  0.0 36.3 jit_solution(4214863353046684475)
XLA Ops:
  0.0 35.3 %shard_map.37.result = bf16[32,64,128]{2,1,0:T(8,128)(2,1)S(1)} custom-call(bf16[32,64,128]{2,1,0:T(8,128)(2,1)} %bitcast.4, bf16[8,64,128]{2,1,0:T(8,128)(2,1)} %bitcast.5, bf16[8,64,128]{2,1,0:T(8,128)(2,1)} %bitcast.6), custom_call_target="tpu_custom_call" | custom-call | tf_op jit(solution)/shard_map/pallas_call | solution.py:289
  35.4 0.8 %shard_map.38 = bf16[32,64,128]{2,1,0:T(8,128)(2,1)} custom-call(bf16[32,64,128]{2,1,0:T(8,128)(2,1)S(1)} %shard_map.37.result), custom_call_target="tpu_custom_call" | custom-call | tf_op jit(solution)/shard_map/pallas_call | solution.py:323

commit v3 on v0

--- a/solution.py
+++ b/solution.py
@@ -164,7 +164,11 @@
             inverse = 1.0 / jnp.sum(row_sum[r, t], axis=0, keepdims=True)
             result = (acc[r, t] * inverse).astype(BF16)
             for n in range(per_tile):
-                out_send[r, t * per_tile + n] = result[:, n * tokens:(n + 1) * tokens]
+                part = result[:, n * tokens:(n + 1) * tokens]
+                if r:
+                    out_send[r, t * per_tile + n] = part
+                else:
+                    out_ref[my_head * group + t * per_tile + n] = part
 
     row_max[...] = jnp.full_like(row_max, -jnp.inf)
     row_sum[...] = jnp.zeros_like(row_sum)
@@ -245,9 +249,6 @@
                 finish(r)
                 ended += [r] if r else []
             n += 1
-    mine = pltpu.make_async_copy(out_send.at[0], out_ref.at[pl.ds(my_head * group, group)], out_sent.at[0])
-    mine.start()
-
     for r in range(1, MEMBERS):
         out_copy(r, member(r)[1]).wait_recv()
         out_copy(r, my_head).wait_send()
@@ -258,7 +259,12 @@
         for block in range(1, BLOCKS):
             for r in range(MEMBERS):
                 forward(kind, block, r).wait_send()
-    mine.wait()
+
+
+def store_kernel(result, out_ref, stored):
+    copy = pltpu.make_async_copy(result, out_ref, stored)
+    copy.start()
+    copy.wait()
 
 
 def solution(mesh):
@@ -274,11 +280,12 @@
         span = MEMBERS * tokens
         scale = 1.0 / math.sqrt(head_dim) / math.log(2.0)
         hbm = pl.BlockSpec(memory_space=pl.ANY)
+        vmem = pl.BlockSpec(memory_space=pltpu.VMEM)
         out_cols = pl.pallas_call(
             functools.partial(attend_kernel, size_x, size_y, scale),
-            out_shape=jax.ShapeDtypeStruct((num_heads, head_dim, tokens), BF16),
+            out_shape=pltpu.VMEM((num_heads, head_dim, tokens), BF16),
             in_specs=[hbm] * 3,
-            out_specs=hbm,
+            out_specs=vmem,
             scratch_shapes=[
                 pltpu.VMEM((num_heads, head_dim, tokens), BF16),
                 pltpu.VMEM((num_kv, head_dim, tokens), BF16),
@@ -308,6 +315,14 @@
                 has_side_effects=True,
             ),
         )(*(jnp.transpose(x, (1, 2, 0)) for x in (q_local, k_local, v_local)))
+        out_cols = pl.pallas_call(
+            store_kernel,
+            out_shape=jax.ShapeDtypeStruct(out_cols.shape, BF16),
+            in_specs=[vmem],
+            out_specs=hbm,
+            scratch_shapes=[pltpu.SemaphoreType.DMA],
+            compiler_params=pltpu.CompilerParams(vmem_limit_bytes=1024 * 1024),
+        )(pltpu.with_memory_space_constraint(out_cols, pltpu.VMEM))
         return jnp.transpose(out_cols, (2, 0, 1))
 
     return jax.shard_map(

time: 35.3 us -> 34.2 us (0.969)
  local copies, waits for them, and re-layouts: 1.87 us -> 0 us
  Pallas kernels: 33.3 us -> 34 us
    unnamed x1 -> x0, local copies, waits for them, and re-layouts: 1.87 us -> none
    pallas_call x0 -> x1, Pallas kernels: none -> 0.8 us  [local_attention(): pl.pallas_call(store_kernel, out_shape=jax.ShapeDtypeStruct(out_cols.shap...]
where the time goes in v3:
time: 34.2 us
  Pallas kernels  34 us (99%)
    pallas_call x1, Pallas kernels, local_attention(): pl.pallas_call(functools.partial(attend_kernel, size_x, size_y, scale), o...  33.2 us
    pallas_call x1, Pallas kernels, local_attention(): pl.pallas_call(store_kernel, out_shape=jax.ShapeDtypeStruct(out_cols.shap...  0.8 us

profile of v3, /device:TPU:97, one launch (start us, length us, event | category | flops | bytes accessed | tf_op | source)
XLA Modules:
  0.0 34.2 jit_solution(4937573067788621824)
XLA Ops:
  0.0 33.2 %shard_map.37.result = bf16[32,64,128]{2,1,0:T(8,128)(2,1)S(1)} custom-call(bf16[32,64,128]{2,1,0:T(8,128)(2,1)} %bitcast.4, bf16[8,64,128]{2,1,0:T(8,128)(2,1)} %bitcast.5, bf16[8,64,128]{2,1,0:T(8,128)(2,1)} %bitcast.6), custom_call_target="tpu_custom_call" | custom-call | tf_op jit(solution)/shard_map/pallas_call | solution.py:284
  33.2 0.8 %shard_map.38 = bf16[32,64,128]{2,1,0:T(8,128)(2,1)} custom-call(bf16[32,64,128]{2,1,0:T(8,128)(2,1)S(1)} %shard_map.37.result), custom_call_target="tpu_custom_call" | custom-call | tf_op jit(solution)/shard_map/pallas_call | solution.py:318
